TPU v7x, 32 devices: a whole 2x2x4 slice. The times are simulated.
32 devices in a mesh: win: 4 (over y, x), dof: 8 (over z, core).
Axes of the slice: x: 2, y: 2, z: 4, core: 2. Of those that a mesh axis runs over, the one named last changes fastest.
Arguments:
- snapshots: bfloat16 [262144, 256], P('dof', 'win'), may hold values from -6 to 6
- sketch_matrix: bfloat16 [262144, 128], P('dof'), may hold values from -0.01171875 to 0.01171875
- pivots: int32 [8, 64], P('win'), may hold values from 0 to 127
Outputs:
- singular: float32 [8, 64], P('win')
- projections: float32 [8, 64, 32], P('win')
All inputs are finite; a program needn't handle non-finite values.
Results may differ from a plain program's by a relative error of at most 0.0003.
Values sent between devices are 32-bit elements; how exact they have to be, the bound alone decides.
No kernel may reach another device: no remote copies, remote signals or barrier semaphores. Data moves between devices by JAX's collectives and lax.ppermute only.
A program may use at most 64 MiB of HBM per device.

v0:
```python
import math
import jax
import jax.numpy as jnp
from jax import lax
from jax.sharding import PartitionSpec as P

RANK = 64
ORTH_ITERS = 2
HIGHEST_PREC = lax.Precision.HIGHEST


def orthogonal(prefix_grams):
    batch_count = prefix_grams.shape[0]
    sketch_width = prefix_grams.shape[1]
    basis_cols = jnp.broadcast_to(
        jnp.eye(sketch_width, RANK, dtype=jnp.float32), (batch_count, sketch_width, RANK)
    )
    for sweep_index in range(ORTH_ITERS):
        images = jnp.einsum("wij,wjk->wik", prefix_grams, basis_cols, precision=HIGHEST_PREC)
        inner_gram = jnp.einsum("wik,wil->wkl", images, images, precision=HIGHEST_PREC)
        chol_factor = jnp.linalg.cholesky(inner_gram)
        solved = jax.scipy.linalg.solve_triangular(
            chol_factor, jnp.swapaxes(images, 1, 2), lower=True
        )
        basis_cols = jnp.swapaxes(solved, 1, 2)
    return basis_cols


def finish(prefix_grams, basis_cols, window_blocks, pivots):
    images = jnp.einsum("wij,wjk->wik", prefix_grams, basis_cols, precision=HIGHEST_PREC)
    singular = jnp.sqrt(jnp.sum(basis_cols * images, axis=1))
    sketch_width = basis_cols.shape[1]
    pivot_table = (
        pivots[:, :, None] == jnp.arange(sketch_width, dtype=jnp.int32)[None, None, :]
    ).astype(jnp.float32)
    pivot_weight = jnp.einsum(
        "wrk,wkr->wr", pivot_table, basis_cols, precision=HIGHEST_PREC
    ) * math.sqrt(sketch_width)
    projections = (
        jnp.einsum("wkr,wks->wrs", basis_cols, window_blocks, precision=HIGHEST_PREC)
        * pivot_weight[:, :, None]
    )
    return (singular, projections)


def masked_gram(gathered, limit):
    column_ids = lax.iota(jnp.int32, gathered.shape[1])
    keep_mask = (column_ids < limit).astype(jnp.float32)
    return jnp.dot(gathered * keep_mask[None, :], gathered.T, precision=HIGHEST_PREC)


def local(snapshots, sketch_matrix, pivots):
    windows_here = pivots.shape[0]
    sketch_width = sketch_matrix.shape[1]
    local_cols = snapshots.shape[1]
    snap_count = local_cols // windows_here
    win_position = lax.axis_index("win")
    partial_value = lax.dot_general(
        sketch_matrix, snapshots, (((0,), (0,)), ((), ())), preferred_element_type=jnp.float32
    )
    coefficients = lax.psum(partial_value, "dof")
    window_blocks = jnp.transpose(
        coefficients.reshape(sketch_width, windows_here, snap_count), (1, 0, 2)
    )
    window_grams = jnp.einsum("wks,wjs->wkj", window_blocks, window_blocks, precision=HIGHEST_PREC)
    own_prefix = jnp.cumsum(window_grams, axis=0)
    gathered = lax.all_gather(coefficients, "win", axis=1, tiled=True)
    earlier = masked_gram(gathered, win_position * local_cols)
    window_ids = win_position * windows_here + jnp.arange(windows_here, dtype=jnp.int32)
    snap_totals = (snap_count * (window_ids + 1)).astype(jnp.float32)
    identity = jnp.eye(sketch_width, dtype=jnp.float32)
    prefix_grams = identity[None] + (earlier[None] + own_prefix) / snap_totals[:, None, None]
    basis_cols = orthogonal(prefix_grams)
    singular, projections = finish(prefix_grams, basis_cols, window_blocks, pivots)
    return (singular, projections)


def solution(mesh):
    placed = (P("dof", "win"), P("dof", None), P("win", None))
    return jax.shard_map(
        local,
        mesh=mesh,
        in_specs=placed,
        out_specs=(P("win", None), P("win", None, None)),
        check_vma=False,
    )
```

profile of v0, /device:TPU:0, one launch (start us, length us, event | category | flops | bytes accessed | tf_op | source)
XLA Modules:
  0.0 94.3 jit_solution(17351688111466763597)
XLA Ops:
  0.6 0.0 copy-start
  0.6 6.2 %fusion.22 = f32[128,64]{0,1:T(8,128)S(1)} fusion(bf16[32768,64]{0,1:T(8,128)(2,1)} %param.6, bf16[32768,128]{1,0:T(8,128)(2,1)} %param.7), kind=kOutput, calls=%fused_computation.42 | convolution fusion | flops 536870912 | bytes 12615680 | tf_op jit(solution)/shard_map/dot_general | solution.py:58
  6.9 30.3 %psum.7 = f32[128,64]{0,1:T(8,128)S(1)} all-reduce(f32[128,64]{0,1:T(8,128)S(1)} %fusion.22), channel_id=1, replica_groups=mesh['win'=4,'dof'=8] {'dof'}, use_global_device_ids=true, to_apply=%region_0.0 | all-reduce | flops 8192 | bytes 65536 | tf_op jit(solution)/shard_map/psum | solution.py:61
  37.2 8.4 %all_gather.3 = f32[128,256]{0,1:T(8,128)S(1)} all-gather(f32[128,64]{0,1:T(8,128)S(1)} %psum.7), channel_id=1, replica_groups=mesh['win'=4,'dof'=8] {'win'}, dimensions={1}, use_global_device_ids=true | all-gather | bytes 163840 | tf_op jit(solution)/shard_map/all_gather | solution.py:67
  45.6 0.5 fusion.3
  46.1 0.4 fusion.18
  46.5 0.1 fusion.1
  46.6 0.4 fusion.15
  47.0 0.2 fusion.19
  47.2 0.1 copy.8
  47.3 11.7 %custom-call.8 = f32[2,64,64]{2,1,0:T(8,128)S(1)} custom-call(f32[2,64,64]{2,1,0:T(8,128)S(1)} %fusion.12), custom_call_target="Cholesky" | custom-call | tf_op jit(solution)/shard_map/jit(cholesky)/cholesky | solution.py:21
  59.1 0.1 compare_reduce_fusion.1
  59.3 0.1 select_bitcast_fusion.1
  59.3 9.8 %custom-call.9 = f32[2,1,64,64]{2,3,1,0:T(8,128)S(1)} custom-call(f32[2,1,64,64]{3,2,1,0:T(8,128)S(1)} %select_bitcast_fusion.1), custom_call_target="InvertDiagBlocksLowerTriangular" | custom-call | tf_op jit(solution)/shard_map/jit(_solve_triangular)/vmap()/triangular_solve | solution.py:22
  69.2 0.3 fusion.9
  69.5 0.4 fusion.20
  69.8 0.2 fusion.21
  70.1 0.1 copy.9
  70.2 11.7 %custom-call.10 = f32[2,64,64]{2,1,0:T(8,128)S(1)} custom-call(f32[2,64,64]{2,1,0:T(8,128)S(1)} %fusion.8), custom_call_target="Cholesky" | custom-call | tf_op jit(solution)/shard_map/jit(cholesky)/cholesky | solution.py:21
  82.0 0.1 compare_reduce_fusion
  82.1 0.1 select_bitcast_fusion
  82.2 9.8 %custom-call.11 = f32[2,1,64,64]{2,3,1,0:T(8,128)S(1)} custom-call(f32[2,1,64,64]{3,2,1,0:T(8,128)S(1)} %select_bitcast_fusion), custom_call_target="InvertDiagBlocksLowerTriangular" | custom-call | tf_op jit(solution)/shard_map/jit(_solve_triangular)/vmap()/triangular_solve | solution.py:22
  92.0 0.0 copy-done
  92.0 0.4 select_reduce_fusion
  92.4 0.8 convolution_multiply_fusion.1
  93.2 0.4 fusion.2
  93.7 0.6 sqrt.3
  (11 shorter events, 0.1 us)
Async XLA Ops:
  0.6 91.4 %copy-start = (s32[2,64]{1,0:T(2,128)S(1)}, s32[2,64]{1,0:T(2,128)}, u32[]{:S(2)}) copy-start(s32[2,64]{1,0:T(2,128)} %param.8) | copy-start | bytes 1540
where the time goes:
time: 94.5 us; the launch traced here: 94.3 us
  other arithmetic  43.7 us (46%)
  blocking collectives  38.7 us (41%)
  matrix products  10.2 us (11%)
    psum x1, blocking collectives, local(): coefficients = lax.psum(partial_value, 'dof')  30.3 us
    another operation x7, other arithmetic, orthogonal(): chol_factor = jnp.linalg.cholesky(inner_gram)  23.8 us
    another operation x5, other arithmetic, orthogonal(): jax.scipy.linalg.solve_triangular(chol_factor, jnp.swapaxes(images, 1, 2)...  19.8 us
    all_gather x1, blocking collectives, local(): gathered = lax.all_gather(coefficients, 'win', axis=1, tiled=True)  8.45 us
    dot_general x1, matrix products, local(): lax.dot_general(sketch_matrix, snapshots, (((0,), (0,)), ((), ())), prefe...  6.24 us

commit v1 on v0

--- a/solution.py
+++ b/solution.py
@@ -58,7 +58,7 @@
     partial_value = lax.dot_general(
         sketch_matrix, snapshots, (((0,), (0,)), ((), ())), preferred_element_type=jnp.float32
     )
-    coefficients = lax.psum(partial_value, "dof")
+    coefficients = jnp.sum(lax.all_gather(partial_value, "dof"), axis=0)
     window_blocks = jnp.transpose(
         coefficients.reshape(sketch_width, windows_here, snap_count), (1, 0, 2)
     )

time: 94.5 us -> 80.2 us (0.85)
  blocking collectives: 38.7 us -> 24.4 us
    psum x1 -> x0, blocking collectives: 30.3 us -> none  [local(): coefficients = lax.psum(partial_value, 'dof')]
    all_gather x0 -> x1, blocking collectives: none -> 15.9 us  [local(): coefficients = jnp.sum(lax.all_gather(partial_value, 'dof'), axis=0)]
where the time goes in v1:
time: 80.2 us; the launch traced here: 80 us
  other arithmetic  43.8 us (55%)
  blocking collectives  24.4 us (30%)
  matrix products  10.2 us (13%)
  between operations  0.82 us (1%)
    another operation x7, other arithmetic, orthogonal(): chol_factor = jnp.linalg.cholesky(inner_gram)  23.8 us
    another operation x5, other arithmetic, orthogonal(): jax.scipy.linalg.solve_triangular(chol_factor, jnp.swapaxes(images, 1, 2)...  19.8 us
    all_gather x1, blocking collectives, local(): coefficients = jnp.sum(lax.all_gather(partial_value, 'dof'), axis=0)  15.9 us
    all_gather x1, blocking collectives, local(): gathered = lax.all_gather(coefficients, 'win', axis=1, tiled=True)  8.47 us
    dot_general x1, matrix products, local(): lax.dot_general(sketch_matrix, snapshots, (((0,), (0,)), ((), ())), prefe...  6.24 us

profile of v1, /device:TPU:0, one launch (start us, length us, event | category | flops | bytes accessed | tf_op | source)
XLA Modules:
  0.0 80.0 jit_solution(4856855974704492232)
XLA Ops:
  0.6 0.0 copy-start
  0.6 6.2 %fusion.22 = f32[128,64]{0,1:T(8,128)S(1)} fusion(bf16[32768,64]{0,1:T(8,128)(2,1)} %param.6, bf16[32768,128]{1,0:T(8,128)(2,1)} %param.7), kind=kOutput, calls=%fused_computation.43 | convolution fusion | flops 536870912 | bytes 12615680 | tf_op jit(solution)/shard_map/dot_general | solution.py:58
  6.9 15.9 %all-gather = f32[1024,64]{0,1:T(8,128)S(1)} all-gather(f32[128,64]{0,1:T(8,128)S(1)} %fusion.22), channel_id=2, replica_groups=mesh['win'=4,'dof'=8] {'dof'}, dimensions={0}, use_global_device_ids=true | all-gather | bytes 294912 | tf_op jit(solution)/shard_map/all_gather | solution.py:61
  22.9 0.1 bitcast_reduce_fusion
  22.9 8.5 %all_gather.11 = f32[128,256]{0,1:T(8,128)S(1)} all-gather(f32[128,64]{0,1:T(8,128)S(1)} %bitcast_reduce_fusion), channel_id=1, replica_groups=mesh['win'=4,'dof'=8] {'win'}, dimensions={1}, use_global_device_ids=true | all-gather | bytes 163840 | tf_op jit(solution)/shard_map/all_gather | solution.py:67
  31.4 0.5 fusion.3
  31.9 0.4 fusion.18
  32.3 0.1 fusion.1
  32.4 0.4 fusion.15
  32.8 0.2 fusion.19
  33.0 0.1 copy.8
  33.1 11.7 %custom-call.8 = f32[2,64,64]{2,1,0:T(8,128)S(1)} custom-call(f32[2,64,64]{2,1,0:T(8,128)S(1)} %fusion.12), custom_call_target="Cholesky" | custom-call | tf_op jit(solution)/shard_map/jit(cholesky)/cholesky | solution.py:21
  44.9 0.1 compare_reduce_fusion.1
  45.0 0.1 select_bitcast_fusion.1
  45.1 9.8 %custom-call.9 = f32[2,1,64,64]{2,3,1,0:T(8,128)S(1)} custom-call(f32[2,1,64,64]{3,2,1,0:T(8,128)S(1)} %select_bitcast_fusion.1), custom_call_target="InvertDiagBlocksLowerTriangular" | custom-call | tf_op jit(solution)/shard_map/jit(_solve_triangular)/vmap()/triangular_solve | solution.py:22
  54.9 0.3 fusion.9
  55.2 0.4 fusion.20
  55.6 0.2 fusion.21
  55.8 0.1 copy.9
  55.9 11.7 %custom-call.10 = f32[2,64,64]{2,1,0:T(8,128)S(1)} custom-call(f32[2,64,64]{2,1,0:T(8,128)S(1)} %fusion.8), custom_call_target="Cholesky" | custom-call | tf_op jit(solution)/shard_map/jit(cholesky)/cholesky | solution.py:21
  67.7 0.1 compare_reduce_fusion
  67.8 0.1 select_bitcast_fusion
  67.9 9.8 %custom-call.11 = f32[2,1,64,64]{2,3,1,0:T(8,128)S(1)} custom-call(f32[2,1,64,64]{3,2,1,0:T(8,128)S(1)} %select_bitcast_fusion), custom_call_target="InvertDiagBlocksLowerTriangular" | custom-call | tf_op jit(solution)/shard_map/jit(_solve_triangular)/vmap()/triangular_solve | solution.py:22
  77.7 0.0 copy-done
  77.8 0.4 select_reduce_fusion
  78.2 0.8 %convolution_multiply_fusion.1 = f32[2,64,32]{1,2,0:T(8,128)} fusion(f32[2,64,128]{2,1,0:T(8,128)S(1)} %get-tuple-element.5, f32[2,128,32]{1,2,0:T(8,128)S(1)} %bitcast.59, f32[2,64]{1,0:T(2,128)S(1)} %broadcast_multiply_fusion), kind=kOutput, calls=%fused_computation.5 | convolution fusion | flops 6295552 | bytes 115200 | tf_op jit(solution)/shard_map/wkr,wks->wrs/dot_general | solution.py:40
  79.0 0.4 fusion.2
  79.4 0.6 sqrt.3
  (12 shorter events, 0.2 us)
Async XLA Ops:
  0.6 77.1 %copy-start = (s32[2,64]{1,0:T(2,128)S(1)}, s32[2,64]{1,0:T(2,128)}, u32[]{:S(2)}) copy-start(s32[2,64]{1,0:T(2,128)} %param.8) | copy-start | bytes 1540
